TPU v7x, 128 devices: a whole 4x4x4 slice. The times are simulated.
128 devices in a mesh: row: 32 (over y, x, core), col: 4 (over z).
Axes of the slice: x: 4, y: 4, z: 4, core: 2. Of those that a mesh axis runs over, the one named last changes fastest.
Arguments:
- density: float32 [256, 256, 256], P('row', 'col'), may hold values from -5 to 5
- green_octant: float32 [256, 256, 256], P('row', 'col'), may hold values from 0 to 0.25
Outputs:
- potential: float32 [256, 256, 256], P('row', 'col')
All inputs are finite; a program needn't handle non-finite values.
Results may differ from a plain program's by a relative error of at most 0.000092.
Values sent between devices are 32-bit elements; how exact they have to be, the bound alone decides.
A program may use at most 64 MiB of HBM per device.

v0:
```python
import itertools

import jax
import jax.numpy as jnp
import numpy as np
from jax import lax
from jax.experimental import pallas as pl
from jax.experimental.pallas import tpu as pltpu
from jax.sharding import PartitionSpec as P

N = 256
ROWS, COLS = 32, 4
DEVICES = ROWS * COLS
BF16, F32 = jnp.bfloat16, jnp.float32
MESH = pl.DeviceIdType.MESH


def hops(offset):
    return sum(min(step, 4 - step) for step in (offset[0], offset[1], offset[3]))


OFFSETS = [o for o in itertools.product(range(4), range(4), range(2), range(4)) if any(o)]
OFFSETS.sort(key=lambda o: -hops(o))


def split(value):
    high = value.astype(BF16)
    return high, (value - high.astype(F32)).astype(BF16)


def tables():
    wave = np.arange(N)[:, None]
    cell = np.arange(N)[None, :]
    angle = np.pi * (((2 * wave + 1) * cell) % (4 * N)) / (2 * N)
    frame = np.concatenate([np.cos(angle), np.sin(angle)], axis=0)
    even = np.where(cell == 0, 1.0, 2.0) * np.cos(angle)
    out = []
    for table in (frame, frame.T, even, even.T):
        high = table.astype(np.float32).astype(BF16)
        out.append(high)
        out.append((table - high.astype(np.float64)).astype(np.float32).astype(BF16))
    return out


def dot3(a, b, dims=(((1,), (0,)), ((), ()))):
    def one(x, y):
        return lax.dot_general(x, y, dims, preferred_element_type=F32)

    return one(a[0], b[0]) + one(a[0], b[1]) + one(a[1], b[0])


def low_half(shape):
    return lax.broadcasted_iota(jnp.int32, shape, len(shape) - 1) < 64


def exchange_halves(a, b):
    low = low_half(a.shape)
    return (
        jnp.where(low, a, pltpu.roll(b, 64, 1)),
        jnp.where(low, pltpu.roll(a, 64, 1), b),
    )


def kernel(
    dens, green, th, tl, tth, ttl, wh, wl, wth, wtl, out,
    send_k, send_d, recv_k, recv_d, send_i, recv_i, khat, stage, total, send_sem, recv_sem,
):
    row, z = lax.axis_index("row"), lax.axis_index("col")
    y, x, c = row // 8, (row // 2) % 4, row % 2
    mine = z * ROWS + row

    def partners():
        for dy, dx, dc, dz in OFFSETS:
            r = (((y + dy) % 4) * 4 + (x + dx) % 4) * 2 + (c + dc) % 2
            yield r, (z + dz) % 4

    barrier = pltpu.get_barrier_semaphore()
    for r, q in partners():
        pl.semaphore_signal(barrier, inc=1, device_id=(r, q), device_id_type=MESH)

    def tile(ref, slot):
        return ref.at[pl.ds(pl.multiple_of(slot * 8, 8), 8)]

    def send(source, target, index):
        for r, q in partners():
            pltpu.make_async_remote_copy(
                src_ref=tile(source, q * ROWS + r),
                dst_ref=tile(target, mine),
                send_sem=send_sem.at[index],
                recv_sem=recv_sem.at[index],
                device_id=(r, q),
                device_id_type=MESH,
            ).start()
        own = pl.ds(pl.multiple_of(mine * 8, 8), 8)
        target[own, :] = source[own, :]

    def arrived(target, sem):
        most = target.at[pl.ds(0, (DEVICES - 1) * 8)]
        pltpu.make_async_copy(most, most, sem).wait()

    def along_z(table, data, target):
        nt = (((1,), (1,)), ((), ()))
        for t in range(4):
            part = (data[0][128 * t : 128 * t + 128], data[1][128 * t : 128 * t + 128])
            result = dot3(table, part, nt)
            first, second = exchange_halves(result[:128], result[128:])
            target[pl.ds(2 * t, DEVICES, stride=8), :] = first
            target[pl.ds(2 * t + 1, DEVICES, stride=8), :] = second

    def both(high, low, start):
        return tuple(
            jnp.concatenate([r[start : start + 128], r[N + start : N + start + 128]], 0)
            for r in (high, low)
        )

    g = split(green[...].reshape(8 * 64, N))
    along_z((wh[...], wl[...]), g, send_k)
    d = split(dens[...].reshape(8 * 64, N))
    along_z(both(th, tl, 0), d, send_d.at[0])
    pl.semaphore_wait(barrier, DEVICES - 1)
    send(send_k, recv_k, 0)
    send(send_d.at[0], recv_d.at[0], 1)
    along_z(both(th, tl, 128), d, send_d.at[1])
    send(send_d.at[1], recv_d.at[1], 2)

    def planes(ref):
        first, second = [], []
        for t in range(2):
            a = ref[512 * t : 512 * t + 256, :]
            b = ref[512 * t + 256 : 512 * t + 512, :]
            low, high = exchange_halves(a, b)
            first.append(low)
            second.append(high)
        return jnp.concatenate(first, 1), jnp.concatenate(second, 1)

    arrived(recv_k, recv_sem.at[0])
    for half, plane in enumerate(planes(recv_k)):
        along_y = dot3(split(plane), (wth[...], wtl[...]))
        khat[half] = dot3((wh[...], wl[...]), split(along_y)) * F32(1.0 / N**3)

    for half in range(2):
        arrived(recv_d.at[half], recv_sem.at[1 + half])
        done = []
        for plane in planes(recv_d.at[half]):
            along_y = dot3(split(plane), (tth[...], ttl[...]))
            along_x = dot3((th[...], tl[...]), split(along_y))
            k = khat[half]
            k = jnp.concatenate([k, k], 1)
            along_x = along_x * jnp.concatenate([k, k], 0)
            back_x = dot3((tth[...], ttl[...]), split(along_x))
            done.append(dot3(split(back_x), (th[...], tl[...])))
        target = send_i.at[half]
        for t in range(2):
            lanes = slice(128 * t, 128 * t + 128)
            low, high = exchange_halves(done[0][:, lanes], done[1][:, lanes])
            target[512 * t : 512 * t + 256, :] = low
            target[512 * t + 256 : 512 * t + 512, :] = high
        send(target, recv_i.at[half], 3 + half)

    for half in range(2):
        arrived(recv_i.at[half], recv_sem.at[3 + half])
        source = recv_i.at[half]
        table = tuple(
            jnp.concatenate(
                [r[:, 128 * half : 128 * half + 128], r[:, N + 128 * half : N + 128 * half + 128]], 1
            )
            for r in (tth, ttl)
        )
        for t in range(4):
            a = source[pl.ds(2 * t, DEVICES, stride=8), :]
            b = source[pl.ds(2 * t + 1, DEVICES, stride=8), :]
            first, second = exchange_halves(a, b)
            waves = split(jnp.concatenate([first, second], 0))
            part = dot3(table, waves)
            if half == 0:
                total[:, 128 * t : 128 * t + 128] = part
            else:
                part = part + total[:, 128 * t : 128 * t + 128]
                out[2 * t : 2 * t + 2] = part.T.reshape(2, 64, N)

    for index, ref in enumerate([recv_k, recv_d.at[0], recv_d.at[1], recv_i.at[0], recv_i.at[1]]):
        arrived(ref, send_sem.at[index])


def solution(mesh):
    constants = tables()

    def on_device(density, green_octant):
        vmem = pl.BlockSpec(memory_space=pltpu.VMEM)
        one = pltpu.VMEM((DEVICES * 8, 128), F32)
        two = pltpu.VMEM((2, DEVICES * 8, 128), F32)
        return pl.pallas_call(
            kernel,
            out_shape=jax.ShapeDtypeStruct((8, 64, N), F32),
            in_specs=[vmem] * (2 + len(constants)),
            out_specs=vmem,
            scratch_shapes=[
                one, two, one, two, two, two,
                pltpu.VMEM((2, N, N), F32),
                pltpu.VMEM((8, 128), F32),
                pltpu.VMEM((N, 512), F32),
                pltpu.SemaphoreType.DMA((5,)),
                pltpu.SemaphoreType.DMA((5,)),
            ],
            compiler_params=pltpu.CompilerParams(
                collective_id=0, has_side_effects=True, vmem_limit_bytes=56 << 20
            ),
        )(density, green_octant, *[jnp.asarray(t) for t in constants])

    return jax.shard_map(
        on_device,
        mesh=mesh,
        in_specs=(P("row", "col", None), P("row", "col", None)),
        out_specs=P("row", "col", None),
        check_vma=False,
    )
```

profile of v0, /device:TPU:1, one launch (start us, length us, event | category | flops | bytes accessed | tf_op | source)
XLA Modules:
  0.0 52.0 jit_solution(8667282104173979639)
XLA Ops:
  0.0 50.1 %shard_map.100 = f32[8,64,256]{2,1,0:T(8,128)} custom-call(f32[8,64,256]{2,1,0:T(8,128)} %dens.1, f32[8,64,256]{2,1,0:T(8,128)} %green.1, bf16[512,256]{1,0:T(8,128)(2,1)} %constant.16.clone.th, bf16[512,256]{1,0:T(8,128)(2,1)} %constant.17.clone.tl, bf16[256,512]{1,0:T(8,128)(2,1)} %constant.18.clone.tth, bf16[256,512]{1,0:T(8,128)(2,1)} %constant.19.clone.ttl, ...), custom_call_target="tpu_custom_call" | custom-call | tf_op jit(solution)/shard_map/pallas_call | solution.py:192
  50.1 1.9 %copy.12 = f32[8,64,256]{2,1,0:T(8,128)} copy(f32[8,64,256]{2,1,0:T(8,128)} %shard_map.100) | data formatting | bytes 1048576
where the time goes:
time: 52.2 us; the launch traced here: 52 us
  Pallas kernels  50.1 us (96%)
  local copies, waits for them, and re-layouts  1.87 us (4%)
    pallas_call x1, Pallas kernels, on_device(): pl.pallas_call(kernel, out_shape=jax.ShapeDtypeStruct((8, 64, N), F32), i...  50.1 us
    unnamed x1, local copies, waits for them, and re-layouts  1.87 us

commit v1 on v0

--- a/solution.py
+++ b/solution.py
@@ -13,6 +13,7 @@
 DEVICES = ROWS * COLS
 BF16, F32 = jnp.bfloat16, jnp.float32
 MESH = pl.DeviceIdType.MESH
+DENS, GREEN, TH, TL, TTH, TTL, WH, WL, WTH, WTL = range(10)
 
 
 def hops(offset):
@@ -61,10 +62,11 @@
     )
 
 
-def kernel(
-    dens, green, th, tl, tth, ttl, wh, wl, wth, wtl, out,
-    send_k, send_d, recv_k, recv_d, send_i, recv_i, khat, stage, total, send_sem, recv_sem,
-):
+def kernel(*refs):
+    operands, out, refs = refs[:10], refs[10], refs[11:]
+    fetched, refs = refs[:10], refs[10:]
+    send_f, recv_f, send_i, recv_i, khat, stage, total, send_sem, recv_sem, load_sem = refs
+    dens, green, th, tl, tth, ttl, wh, wl, wth, wtl = fetched
     row, z = lax.axis_index("row"), lax.axis_index("col")
     y, x, c = row // 8, (row // 2) % 4, row % 2
     mine = z * ROWS + row
@@ -75,8 +77,16 @@
             yield r, (z + dz) % 4
 
     barrier = pltpu.get_barrier_semaphore()
+    def load(index):
+        return pltpu.make_async_copy(operands[index], fetched[index], load_sem.at[index])
+
+    order = (DENS, TH, TL, GREEN, WH, WL, WTH, WTL, TTH, TTL)
+    for index in order[:3]:
+        load(index).start()
     for r, q in partners():
         pl.semaphore_signal(barrier, inc=1, device_id=(r, q), device_id_type=MESH)
+    for index in order[3:]:
+        load(index).start()
 
     def tile(ref, slot):
         return ref.at[pl.ds(pl.multiple_of(slot * 8, 8), 8)]
@@ -98,30 +108,33 @@
         most = target.at[pl.ds(0, (DEVICES - 1) * 8)]
         pltpu.make_async_copy(most, most, sem).wait()
 
-    def along_z(table, data, target):
-        nt = (((1,), (1,)), ((), ()))
+    def along_z(upper, lower, target):
+        def one(pair, t):
+            rows = slice(128 * t, 128 * t + 128)
+            data = tuple(ref[rows] for ref in pair[1])
+            return dot3(pair[0], data, (((1,), (1,)), ((), ())))
+
         for t in range(4):
-            part = (data[0][128 * t : 128 * t + 128], data[1][128 * t : 128 * t + 128])
-            result = dot3(table, part, nt)
-            first, second = exchange_halves(result[:128], result[128:])
+            first, second = exchange_halves(one(upper, t), one(lower, t))
             target[pl.ds(2 * t, DEVICES, stride=8), :] = first
             target[pl.ds(2 * t + 1, DEVICES, stride=8), :] = second
 
-    def both(high, low, start):
-        return tuple(
-            jnp.concatenate([r[start : start + 128], r[N + start : N + start + 128]], 0)
-            for r in (high, low)
-        )
-
+    def rows_of(high, low, start):
+        return high[start : start + 128], low[start : start + 128]
+
+    for index in order[:6]:
+        load(index).wait()
     g = split(green[...].reshape(8 * 64, N))
-    along_z((wh[...], wl[...]), g, send_k)
     d = split(dens[...].reshape(8 * 64, N))
-    along_z(both(th, tl, 0), d, send_d.at[0])
+    along_z((rows_of(th, tl, 0), d), (rows_of(wh, wl, 0), g), send_f.at[0])
     pl.semaphore_wait(barrier, DEVICES - 1)
-    send(send_k, recv_k, 0)
-    send(send_d.at[0], recv_d.at[0], 1)
-    along_z(both(th, tl, 128), d, send_d.at[1])
-    send(send_d.at[1], recv_d.at[1], 2)
+    send(send_f.at[0], recv_f.at[0], 0)
+    along_z((rows_of(th, tl, N), d), (rows_of(wh, wl, 128), g), send_f.at[1])
+    send(send_f.at[1], recv_f.at[1], 1)
+    along_z((rows_of(th, tl, 128), d), (rows_of(th, tl, N + 128), d), send_f.at[2])
+    send(send_f.at[2], recv_f.at[2], 2)
+    for index in order[6:]:
+        load(index).wait()
 
     def planes(ref):
         first, second = [], []
@@ -133,29 +146,39 @@
             second.append(high)
         return jnp.concatenate(first, 1), jnp.concatenate(second, 1)
 
-    arrived(recv_k, recv_sem.at[0])
-    for half, plane in enumerate(planes(recv_k)):
+    def transform_kernel(half, plane):
         along_y = dot3(split(plane), (wth[...], wtl[...]))
         khat[half] = dot3((wh[...], wl[...]), split(along_y)) * F32(1.0 / N**3)
 
-    for half in range(2):
-        arrived(recv_d.at[half], recv_sem.at[1 + half])
-        done = []
-        for plane in planes(recv_d.at[half]):
-            along_y = dot3(split(plane), (tth[...], ttl[...]))
-            along_x = dot3((th[...], tl[...]), split(along_y))
-            k = khat[half]
-            k = jnp.concatenate([k, k], 1)
-            along_x = along_x * jnp.concatenate([k, k], 0)
-            back_x = dot3((tth[...], ttl[...]), split(along_x))
-            done.append(dot3(split(back_x), (th[...], tl[...])))
+    def convolve(half, plane):
+        along_y = dot3(split(plane), (tth[...], ttl[...]))
+        along_x = dot3((th[...], tl[...]), split(along_y))
+        k = khat[half]
+        k = jnp.concatenate([k, k], 1)
+        along_x = along_x * jnp.concatenate([k, k], 0)
+        back_x = dot3((tth[...], ttl[...]), split(along_x))
+        return dot3(split(back_x), (th[...], tl[...]))
+
+    def send_back(half, cosine, sine):
         target = send_i.at[half]
         for t in range(2):
             lanes = slice(128 * t, 128 * t + 128)
-            low, high = exchange_halves(done[0][:, lanes], done[1][:, lanes])
+            low, high = exchange_halves(cosine[:, lanes], sine[:, lanes])
             target[512 * t : 512 * t + 256, :] = low
             target[512 * t + 256 : 512 * t + 512, :] = high
         send(target, recv_i.at[half], 3 + half)
+
+    arrived(recv_f.at[0], recv_sem.at[0])
+    plane, plane_k = planes(recv_f.at[0])
+    transform_kernel(0, plane_k)
+    stage[...] = convolve(0, plane)
+    arrived(recv_f.at[1], recv_sem.at[1])
+    plane, plane_k = planes(recv_f.at[1])
+    send_back(0, stage[...], convolve(0, plane))
+    transform_kernel(1, plane_k)
+    arrived(recv_f.at[2], recv_sem.at[2])
+    plane, other = planes(recv_f.at[2])
+    send_back(1, convolve(1, plane), convolve(1, other))
 
     for half in range(2):
         arrived(recv_i.at[half], recv_sem.at[3 + half])
@@ -178,8 +201,8 @@
                 part = part + total[:, 128 * t : 128 * t + 128]
                 out[2 * t : 2 * t + 2] = part.T.reshape(2, 64, N)
 
-    for index, ref in enumerate([recv_k, recv_d.at[0], recv_d.at[1], recv_i.at[0], recv_i.at[1]]):
-        arrived(ref, send_sem.at[index])
+    for index in range(5):
+        arrived(recv_i.at[0], send_sem.at[index])
 
 
 def solution(mesh):
@@ -187,25 +210,28 @@
 
     def on_device(density, green_octant):
         vmem = pl.BlockSpec(memory_space=pltpu.VMEM)
-        one = pltpu.VMEM((DEVICES * 8, 128), F32)
+        operands = [density, green_octant, *[jnp.asarray(t) for t in constants]]
+        three = pltpu.VMEM((3, DEVICES * 8, 128), F32)
         two = pltpu.VMEM((2, DEVICES * 8, 128), F32)
         return pl.pallas_call(
             kernel,
-            out_shape=jax.ShapeDtypeStruct((8, 64, N), F32),
-            in_specs=[vmem] * (2 + len(constants)),
+            out_shape=pltpu.VMEM((8, 64, N), F32),
+            in_specs=[pl.BlockSpec(memory_space=pl.ANY)] * len(operands),
             out_specs=vmem,
             scratch_shapes=[
-                one, two, one, two, two, two,
+                *[pltpu.VMEM(o.shape, o.dtype) for o in operands],
+                three, three, two, two,
                 pltpu.VMEM((2, N, N), F32),
-                pltpu.VMEM((8, 128), F32),
+                pltpu.VMEM((N, N), F32),
                 pltpu.VMEM((N, 512), F32),
                 pltpu.SemaphoreType.DMA((5,)),
                 pltpu.SemaphoreType.DMA((5,)),
+                pltpu.SemaphoreType.DMA((len(operands),)),
             ],
             compiler_params=pltpu.CompilerParams(
                 collective_id=0, has_side_effects=True, vmem_limit_bytes=56 << 20
             ),
-        )(density, green_octant, *[jnp.asarray(t) for t in constants])
+        )(*operands)
 
     return jax.shard_map(
         on_device,

time: 52.2 us -> 46.3 us (0.89)
  Pallas kernels: 50.1 us -> 45 us
  local copies, waits for them, and re-layouts: 1.87 us -> 0.8 us
    pallas_call x1, Pallas kernels: 50.1 us -> 45 us  [on_device(): pl.pallas_call(kernel, out_shape=pltpu.VMEM((8, 64, N), F32), in_specs=[p...]
    unnamed x1, local copies, waits for them, and re-layouts: 1.87 us -> 0.8 us
where the time goes in v1:
time: 46.3 us; the launch traced here: 45.8 us
  Pallas kernels  45 us (97%)
  local copies, waits for them, and re-layouts  0.8 us (2%)
    pallas_call x1, Pallas kernels, on_device(): pl.pallas_call(kernel, out_shape=pltpu.VMEM((8, 64, N), F32), in_specs=[p...  45 us

profile of v1, /device:TPU:1, one launch (start us, length us, event | category | flops | bytes accessed | tf_op | source)
XLA Modules:
  0.0 45.8 jit_solution(17469097452008923877)
XLA Ops:
  0.0 45.0 %shard_map.100 = f32[8,64,256]{2,1,0:T(8,128)S(1)} custom-call(f32[8,64,256]{2,1,0:T(8,128)} %refs_0_.1, f32[8,64,256]{2,1,0:T(8,128)} %refs_1_.1, bf16[512,256]{1,0:T(8,128)(2,1)} %constant.16.clone.refs_2_, bf16[512,256]{1,0:T(8,128)(2,1)} %constant.17.clone.refs_3_, bf16[256,512]{1,0:T(8,128)(2,1)} %constant.18.clone.refs_4_, ...), custom_call_target="tpu_custom_call" | custom-call | tf_op jit(solution)/shard_map/pallas_call | solution.py:216
  45.0 0.8 %copy.12 = f32[8,64,256]{2,1,0:T(8,128)} copy(f32[8,64,256]{2,1,0:T(8,128)S(1)} %shard_map.100) | data formatting | bytes 1048576

commit v2 on v1

--- a/solution.py
+++ b/solution.py
@@ -1,4 +1,5 @@
 import itertools
+import random
 
 import jax
 import jax.numpy as jnp
@@ -13,15 +14,33 @@
 DEVICES = ROWS * COLS
 BF16, F32 = jnp.bfloat16, jnp.float32
 MESH = pl.DeviceIdType.MESH
-DENS, GREEN, TH, TL, TTH, TTL, WH, WL, WTH, WTL = range(10)
-
-
-def hops(offset):
-    return sum(min(step, 4 - step) for step in (offset[0], offset[1], offset[3]))
-
-
-OFFSETS = [o for o in itertools.product(range(4), range(4), range(2), range(4)) if any(o)]
-OFFSETS.sort(key=lambda o: -hops(o))
+DENS, GREEN, TH, TL, TTH, TTL, WH, WL, WTH, WTL, XWH, XWL, XF, XFL, XIH, XIL = range(16)
+
+
+def steps(offset):
+    taken = np.zeros((3, 2))
+    for dim, step in enumerate((offset[0], offset[1], offset[3])):
+        if step == 2:
+            taken[dim] += 1
+        elif step:
+            taken[dim, step // 2] += 1
+    return taken
+
+
+def send_order(seed, window=40):
+    rest = [o for o in itertools.product(range(4), range(4), range(2), range(4)) if any(o)]
+    random.Random(seed).shuffle(rest)
+    rest.sort(key=lambda o: -sum(min(n, 4 - n) for n in (o[0], o[1], o[3])))
+    load, order = np.zeros((3, 2)), []
+    while rest:
+        best = min(rest[:window], key=lambda o: ((load + steps(o)).max(), (load + steps(o)).var()))
+        rest.remove(best)
+        load += steps(best)
+        order.append(best)
+    return order
+
+
+ORDERS = [send_order(5 + chunk) for chunk in range(5)]
 
 
 def split(value):
@@ -35,12 +54,21 @@
     angle = np.pi * (((2 * wave + 1) * cell) % (4 * N)) / (2 * N)
     frame = np.concatenate([np.cos(angle), np.sin(angle)], axis=0)
     even = np.where(cell == 0, 1.0, 2.0) * np.cos(angle)
+    folded = np.concatenate([np.arange(N // 2), np.arange(N - 1, N // 2 - 1, -1)])
+    middle = np.pi * (((2 * wave + 1) * (2 * cell[:, : N // 2] - (N - 1))) % (8 * N)) / (4 * N)
+    half = np.concatenate([np.cos(middle), np.sin(middle)], axis=0)
+
+    def terms(table):
+        high = table.astype(np.float32).astype(BF16)
+        return [high, (table - high.astype(np.float64)).astype(np.float32).astype(BF16)]
+
     out = []
-    for table in (frame, frame.T, even, even.T):
-        high = table.astype(np.float32).astype(BF16)
-        out.append(high)
-        out.append((table - high.astype(np.float64)).astype(np.float32).astype(BF16))
-    return out
+    for table in (frame, frame.T, even, even.T, even[:, folded]):
+        out += terms(table)
+    high, low = terms(half)
+    out += [np.concatenate([high, high], axis=1), low]
+    high, low = terms(np.concatenate([np.cos(middle).T, np.sin(middle).T], axis=1))
+    return [*out, high, low]
 
 
 def dot3(a, b, dims=(((1,), (0,)), ((), ()))):
@@ -63,16 +91,24 @@
 
 
 def kernel(*refs):
-    operands, out, refs = refs[:10], refs[10], refs[11:]
-    fetched, refs = refs[:10], refs[10:]
-    send_f, recv_f, send_i, recv_i, khat, stage, total, send_sem, recv_sem, load_sem = refs
-    dens, green, th, tl, tth, ttl, wh, wl, wth, wtl = fetched
+    operands, out, refs = refs[:16], refs[16], refs[17:]
+    fetched, refs = refs[:16], refs[16:]
+    send_f, recv_f, send_i, recv_i, khat, stage, waves, total, send_sem, recv_sem, load_sem = refs
+    dens, green, th, tl, tth, ttl, wh, wl, wth, wtl, xwh, xwl, xf, xfl, xih, xil = fetched
     row, z = lax.axis_index("row"), lax.axis_index("col")
     y, x, c = row // 8, (row // 2) % 4, row % 2
-    mine = z * ROWS + row
-
-    def partners():
-        for dy, dx, dc, dz in OFFSETS:
+    flip = row // 16
+
+    def slot(r, q):
+        return q * ROWS + r + (r // 16) * (47 - 2 * r)
+
+    def line(n):
+        return n + flip * (7 - 2 * n)
+
+    mine = slot(row, z)
+
+    def partners(chunk=0):
+        for dy, dx, dc, dz in ORDERS[chunk]:
             r = (((y + dy) % 4) * 4 + (x + dx) % 4) * 2 + (c + dc) % 2
             yield r, (z + dz) % 4
 
@@ -80,7 +116,7 @@
     def load(index):
         return pltpu.make_async_copy(operands[index], fetched[index], load_sem.at[index])
 
-    order = (DENS, TH, TL, GREEN, WH, WL, WTH, WTL, TTH, TTL)
+    order = (DENS, TH, TL, GREEN, WH, WL, WTH, WTL, XWH, XWL, TTH, TTL, XF, XFL, XIH, XIL)
     for index in order[:3]:
         load(index).start()
     for r, q in partners():
@@ -88,13 +124,13 @@
     for index in order[3:]:
         load(index).start()
 
-    def tile(ref, slot):
-        return ref.at[pl.ds(pl.multiple_of(slot * 8, 8), 8)]
+    def tile(ref, index):
+        return ref.at[pl.ds(pl.multiple_of(index * 8, 8), 8)]
 
     def send(source, target, index):
-        for r, q in partners():
+        for r, q in partners(index):
             pltpu.make_async_remote_copy(
-                src_ref=tile(source, q * ROWS + r),
+                src_ref=tile(source, slot(r, q)),
                 dst_ref=tile(target, mine),
                 send_sem=send_sem.at[index],
                 recv_sem=recv_sem.at[index],
@@ -116,8 +152,8 @@
 
         for t in range(4):
             first, second = exchange_halves(one(upper, t), one(lower, t))
-            target[pl.ds(2 * t, DEVICES, stride=8), :] = first
-            target[pl.ds(2 * t + 1, DEVICES, stride=8), :] = second
+            target[pl.ds(line(2 * t), DEVICES, stride=8), :] = first
+            target[pl.ds(line(2 * t + 1), DEVICES, stride=8), :] = second
 
     def rows_of(high, low, start):
         return high[start : start + 128], low[start : start + 128]
@@ -129,9 +165,9 @@
     along_z((rows_of(th, tl, 0), d), (rows_of(wh, wl, 0), g), send_f.at[0])
     pl.semaphore_wait(barrier, DEVICES - 1)
     send(send_f.at[0], recv_f.at[0], 0)
-    along_z((rows_of(th, tl, N), d), (rows_of(wh, wl, 128), g), send_f.at[1])
+    along_z((rows_of(th, tl, N), d), (rows_of(th, tl, 128), d), send_f.at[1])
     send(send_f.at[1], recv_f.at[1], 1)
-    along_z((rows_of(th, tl, 128), d), (rows_of(th, tl, N + 128), d), send_f.at[2])
+    along_z((rows_of(th, tl, N + 128), d), (rows_of(wh, wl, 128), g), send_f.at[2])
     send(send_f.at[2], recv_f.at[2], 2)
     for index in order[6:]:
         load(index).wait()
@@ -148,16 +184,27 @@
 
     def transform_kernel(half, plane):
         along_y = dot3(split(plane), (wth[...], wtl[...]))
-        khat[half] = dot3((wh[...], wl[...]), split(along_y)) * F32(1.0 / N**3)
-
-    def convolve(half, plane):
+        khat[half] = dot3((xwh[...], xwl[...]), split(along_y)) * F32(1.0 / N**3)
+
+    def ahead(plane):
         along_y = dot3(split(plane), (tth[...], ttl[...]))
-        along_x = dot3((th[...], tl[...]), split(along_y))
+        upper, lower = along_y[: N // 2], along_y[N // 2 :]
+
+        def along_x(start, cells):
+            high, low = split(cells)
+            rows = slice(start, start + N)
+            return jnp.dot(
+                xf[rows, :], jnp.concatenate([high, low], 0), preferred_element_type=F32
+            ) + jnp.dot(xfl[rows, :], high, preferred_element_type=F32)
+
+        return along_x(0, upper + lower), along_x(N, upper - lower)
+
+    def back(half, cosine, sine):
         k = khat[half]
         k = jnp.concatenate([k, k], 1)
-        along_x = along_x * jnp.concatenate([k, k], 0)
-        back_x = dot3((tth[...], ttl[...]), split(along_x))
-        return dot3(split(back_x), (th[...], tl[...]))
+        even = dot3((xih[:, :N], xil[:, :N]), split(cosine * k))
+        odd = dot3((xih[:, N:], xil[:, N:]), split(sine * k))
+        return dot3(split(jnp.concatenate([even + odd, even - odd], 0)), (th[...], tl[...]))
 
     def send_back(half, cosine, sine):
         target = send_i.at[half]
@@ -171,14 +218,15 @@
     arrived(recv_f.at[0], recv_sem.at[0])
     plane, plane_k = planes(recv_f.at[0])
     transform_kernel(0, plane_k)
-    stage[...] = convolve(0, plane)
+    stage[...] = back(0, *ahead(plane))
     arrived(recv_f.at[1], recv_sem.at[1])
-    plane, plane_k = planes(recv_f.at[1])
-    send_back(0, stage[...], convolve(0, plane))
+    plane, other = planes(recv_f.at[1])
+    send_back(0, stage[...], back(0, *ahead(plane)))
+    waves[0], waves[1] = ahead(other)
+    arrived(recv_f.at[2], recv_sem.at[2])
+    plane, plane_k = planes(recv_f.at[2])
     transform_kernel(1, plane_k)
-    arrived(recv_f.at[2], recv_sem.at[2])
-    plane, other = planes(recv_f.at[2])
-    send_back(1, convolve(1, plane), convolve(1, other))
+    send_back(1, back(1, waves[0], waves[1]), back(1, *ahead(plane)))
 
     for half in range(2):
         arrived(recv_i.at[half], recv_sem.at[3 + half])
@@ -190,8 +238,8 @@
             for r in (tth, ttl)
         )
         for t in range(4):
-            a = source[pl.ds(2 * t, DEVICES, stride=8), :]
-            b = source[pl.ds(2 * t + 1, DEVICES, stride=8), :]
+            a = source[pl.ds(line(2 * t), DEVICES, stride=8), :]
+            b = source[pl.ds(line(2 * t + 1), DEVICES, stride=8), :]
             first, second = exchange_halves(a, b)
             waves = split(jnp.concatenate([first, second], 0))
             part = dot3(table, waves)
@@ -223,7 +271,8 @@
                 three, three, two, two,
                 pltpu.VMEM((2, N, N), F32),
                 pltpu.VMEM((N, N), F32),
-                pltpu.VMEM((N, 512), F32),
+                pltpu.VMEM((2, N, 2 * N), F32),
+                pltpu.VMEM((N, 2 * N), F32),
                 pltpu.SemaphoreType.DMA((5,)),
                 pltpu.SemaphoreType.DMA((5,)),
                 pltpu.SemaphoreType.DMA((len(operands),)),

time: 46.3 us -> 44.9 us (0.970)
  Pallas kernels: 45 us -> 43.9 us
    pallas_call x1, Pallas kernels: 45 us -> 43.9 us  [on_device(): pl.pallas_call(kernel, out_shape=pltpu.VMEM((8, 64, N), F32), in_specs=[p...]
where the time goes in v2:
time: 44.9 us; the launch traced here: 44.8 us
  Pallas kernels  43.9 us (98%)
  local copies, waits for them, and re-layouts  0.8 us (2%)
    pallas_call x1, Pallas kernels, on_device(): pl.pallas_call(kernel, out_shape=pltpu.VMEM((8, 64, N), F32), in_specs=[p...  43.9 us

profile of v2, /device:TPU:1, one launch (start us, length us, event | category | flops | bytes accessed | tf_op | source)
XLA Modules:
  0.0 44.8 jit_solution(747810367808845393)
XLA Ops:
  0.0 43.9 %shard_map.154 = f32[8,64,256]{2,1,0:T(8,128)S(1)} custom-call(f32[8,64,256]{2,1,0:T(8,128)} %refs_0_.1, f32[8,64,256]{2,1,0:T(8,128)} %refs_1_.1, bf16[512,256]{1,0:T(8,128)(2,1)} %constant.28.clone.refs_2_, bf16[512,256]{1,0:T(8,128)(2,1)} %constant.29.clone.refs_3_, bf16[256,512]{1,0:T(8,128)(2,1)} %constant.30.clone.refs_4_, ...), custom_call_target="tpu_custom_call" | custom-call | tf_op jit(solution)/shard_map/pallas_call | solution.py:264
  44.0 0.8 %copy.18 = f32[8,64,256]{2,1,0:T(8,128)} copy(f32[8,64,256]{2,1,0:T(8,128)S(1)} %shard_map.154) | data formatting | bytes 1048576

commit v3 on v2

--- a/solution.py
+++ b/solution.py
@@ -40,6 +40,7 @@
     return order
 
 
+LATE = (3, 4)
 ORDERS = [send_order(5 + chunk) for chunk in range(5)]
 
 
@@ -127,16 +128,33 @@
     def tile(ref, index):
         return ref.at[pl.ds(pl.multiple_of(index * 8, 8), 8)]
 
+    def ordered(index):
+        if index not in LATE:
+            yield from ((r, q, False) for r, q in partners(index))
+            return
+        for base in (0, 2):
+            for dy, dx, dc, dz in ORDERS[index] + [(0, 0, 0, 0)]:
+                if dz < 2:
+                    r = (((y + dy) % 4) * 4 + (x + dx) % 4) * 2 + (c + dc) % 2
+                    yield r, base + (z + dz) % 2, (dy, dx, dc) == (0, 0, 0)
+
     def send(source, target, index):
-        for r, q in partners(index):
-            pltpu.make_async_remote_copy(
-                src_ref=tile(source, slot(r, q)),
-                dst_ref=tile(target, mine),
-                send_sem=send_sem.at[index],
-                recv_sem=recv_sem.at[index],
-                device_id=(r, q),
-                device_id_type=MESH,
-            ).start()
+        for r, q, near in ordered(index):
+
+            def start(r=r, q=q):
+                pltpu.make_async_remote_copy(
+                    src_ref=tile(source, slot(r, q)),
+                    dst_ref=tile(target, mine),
+                    send_sem=send_sem.at[index],
+                    recv_sem=recv_sem.at[index],
+                    device_id=(r, q),
+                    device_id_type=MESH,
+                ).start()
+
+            if near:
+                pl.when(q != z)(start)
+            else:
+                start()
         own = pl.ds(pl.multiple_of(mine * 8, 8), 8)
         target[own, :] = source[own, :]
 

time: 44.9 us -> 44.1 us (0.982)
  Pallas kernels: 43.9 us -> 43.2 us
    pallas_call x1, Pallas kernels: 43.9 us -> 43.2 us  [on_device(): pl.pallas_call(kernel, out_shape=pltpu.VMEM((8, 64, N), F32), in_specs=[p...]
where the time goes in v3:
time: 44.1 us; the launch traced here: 44 us
  Pallas kernels  43.2 us (98%)
  local copies, waits for them, and re-layouts  0.8 us (2%)
    pallas_call x1, Pallas kernels, on_device(): pl.pallas_call(kernel, out_shape=pltpu.VMEM((8, 64, N), F32), in_specs=[p...  43.2 us

profile of v3, /device:TPU:1, one launch (start us, length us, event | category | flops | bytes accessed | tf_op | source)
XLA Modules:
  0.0 44.0 jit_solution(11851530231182718155)
XLA Ops:
  0.0 43.2 %shard_map.154 = f32[8,64,256]{2,1,0:T(8,128)S(1)} custom-call(f32[8,64,256]{2,1,0:T(8,128)} %refs_0_.1, f32[8,64,256]{2,1,0:T(8,128)} %refs_1_.1, bf16[512,256]{1,0:T(8,128)(2,1)} %constant.28.clone.refs_2_, bf16[512,256]{1,0:T(8,128)(2,1)} %constant.29.clone.refs_3_, bf16[256,512]{1,0:T(8,128)(2,1)} %constant.30.clone.refs_4_, ...), custom_call_target="tpu_custom_call" | custom-call | tf_op jit(solution)/shard_map/pallas_call | solution.py:282
  43.2 0.8 %copy.18 = f32[8,64,256]{2,1,0:T(8,128)} copy(f32[8,64,256]{2,1,0:T(8,128)S(1)} %shard_map.154) | data formatting | bytes 1048576

commit v4 on v3

--- a/solution.py
+++ b/solution.py
@@ -40,7 +40,7 @@
     return order
 
 
-LATE = (3, 4)
+LATE = (2, 3, 4)
 ORDERS = [send_order(5 + chunk) for chunk in range(5)]
 
 

time: 44.1 us -> 46.4 us (1.052)
  the two profiles are of different devices: /device:TPU:1 before, /device:TPU:64 now
where the time goes in v4:
time: 46.4 us; the launch traced here: 46.3 us
  Pallas kernels  45.5 us (98%)
  local copies, waits for them, and re-layouts  0.8 us (2%)
    pallas_call x1, Pallas kernels, on_device(): pl.pallas_call(kernel, out_shape=pltpu.VMEM((8, 64, N), F32), in_specs=[p...  45.5 us

profile of v4, /device:TPU:64, one launch (start us, length us, event | category | flops | bytes accessed | tf_op | source)
XLA Modules:
  0.0 46.3 jit_solution(10340073329371703194)
XLA Ops:
  0.0 45.5 %shard_map.154 = f32[8,64,256]{2,1,0:T(8,128)S(1)} custom-call(f32[8,64,256]{2,1,0:T(8,128)} %refs_0_.1, f32[8,64,256]{2,1,0:T(8,128)} %refs_1_.1, bf16[512,256]{1,0:T(8,128)(2,1)} %constant.28.clone.refs_2_, bf16[512,256]{1,0:T(8,128)(2,1)} %constant.29.clone.refs_3_, bf16[256,512]{1,0:T(8,128)(2,1)} %constant.30.clone.refs_4_, ...), custom_call_target="tpu_custom_call" | custom-call | tf_op jit(solution)/shard_map/pallas_call | solution.py:282
  45.5 0.8 %copy.18 = f32[8,64,256]{2,1,0:T(8,128)} copy(f32[8,64,256]{2,1,0:T(8,128)S(1)} %shard_map.154) | data formatting | bytes 1048576
